TPU v7x, 32 devices: a whole 2x2x4 slice. The times are simulated.
32 devices in a mesh: row: 4 (over z), col: 8 (over y, x, core).
Axes of the slice: x: 2, y: 2, z: 4, core: 2. Of those that a mesh axis runs over, the one named last changes fastest.
Arguments:
- matrix: float32 [15360, 15360], P('row', 'col'), may hold values from -4 to 4
- rhs: float32 [15360, 4096], P('row', 'col'), may hold values from -6 to 6
- pivot_inverses: bfloat16 [2, 512, 512], replicated, may hold values from -0.046875 to 0.046875
- panel_order: int32 [2], replicated, may hold values from 0 to 29, as said below
Outputs:
- factored: bfloat16 [15360, 15360], P('row', 'col')
- updated_rhs: float32 [15360, 4096], P('row', 'col')
- rhs_norms: float32 [4096], P('col')
Inputs may be any that keep to these rules, and one draw needn't show every extreme that they name: `panel_order`: two different panel indices, one of which is the last panel, 29.
All inputs are finite; a program needn't handle non-finite values.
Results may differ from a plain program's by a relative error of at most 0.001.
Values sent between devices are 32-bit elements; how exact they have to be, the bound alone decides.
No kernel may reach another device: no remote copies, remote signals or barrier semaphores. Data moves between devices by JAX's collectives and lax.ppermute only.
A program may use at most 192 MiB of HBM per device.

v0:
```python
import jax
import jax.numpy as jnp
from jax import lax
from jax.sharding import PartitionSpec as P

N = 15360
PW = 512


def product(first, second):
    return jnp.dot(
        first, second, precision=lax.Precision.HIGHEST, preferred_element_type=jnp.float32
    )


def cut_along(values, start, length, axis_dim):
    return lax.dynamic_slice_in_dim(values, start, length, axis_dim)


def refresh(sub_block, mult_rows, upper_rows, row_keep, col_keep, fresh_col, placed):
    updated = sub_block - row_keep[:, None] * product(mult_rows, upper_rows * col_keep[None, :])
    return jnp.where((row_keep[:, None] > 0) & (fresh_col[None, :] > 0), placed, updated)


def on_device(matrix, rhs, pivot_inverses, panel_order):
    row_count = lax.axis_size("row")
    col_count = lax.axis_size("col")
    block_size = PW // row_count
    group_count = col_count // row_count
    col_index = lax.axis_index("col")
    row_len, col_len = matrix.shape
    row_block_id = jnp.arange(row_len, dtype=jnp.int32) // block_size
    col_block_id = jnp.arange(col_len, dtype=jnp.int32) // block_size

    def column_hit(panel_id):
        is_owner = col_index // row_count == panel_id % group_count
        return (
            ((col_block_id == panel_id // group_count) & is_owner).astype(jnp.float32),
            is_owner,
        )

    def take_slices(current, right_sides, panel_id):
        start = panel_id * block_size
        return (
            cut_along(current, start, block_size, 0),
            cut_along(right_sides, start, block_size, 0),
            cut_along(current, panel_id // group_count * block_size, block_size, 1),
        )

    current = matrix
    right_sides = rhs
    row_piece, rhs_piece, column_slab = take_slices(current, right_sides, panel_order[0])
    for section in range(2):
        panel_id = panel_order[section]
        row_keep = jnp.ones((row_len,), jnp.float32)
        col_keep = jnp.ones((col_len,), jnp.float32)
        for earlier in range(section + 1):
            row_keep = row_keep * (row_block_id != panel_order[earlier]).astype(jnp.float32)
            hit, owner_flag = column_hit(panel_order[earlier])
            col_keep = col_keep * (1.0 - hit)
        fresh_col, keep_is_owner = column_hit(panel_order[section])
        row_keep, col_keep, fresh_col, is_owner = (row_keep, col_keep, fresh_col, keep_is_owner)
        upper_rows, rhs_rows = (
            lax.all_gather(row_piece, "row", axis=0, tiled=True),
            lax.all_gather(rhs_piece, "row", axis=0, tiled=True),
        )
        inverse = pivot_inverses[section].astype(jnp.float32)
        own_rows = cut_along(inverse, col_index % row_count * block_size, block_size, 0)
        partial_value = jnp.where(is_owner, product(column_slab, own_rows), 0.0)
        multipliers = lax.psum(partial_value, "col")
        own_mult = cut_along(multipliers, col_index % row_count * block_size, block_size, 1)
        placed = lax.dynamic_update_slice_in_dim(
            jnp.zeros_like(current), own_mult, panel_id // group_count * block_size, 1
        )
        current = refresh(current, multipliers, upper_rows, row_keep, col_keep, fresh_col, placed)
        right_sides = right_sides - row_keep[:, None] * product(multipliers, rhs_rows)
        if section == 0:
            row_piece, rhs_piece, column_slab = take_slices(current, right_sides, panel_order[1])
    totals = lax.psum(jnp.sum(right_sides * right_sides, axis=0), "row")
    rhs_norms = jnp.sqrt(totals / N + 1e-06)
    return (current.astype(jnp.bfloat16), right_sides, rhs_norms)


def solution(mesh):
    in_specs = (P("row", "col"), P("row", "col"), P(), P())
    out_specs = (P("row", "col"), P("row", "col"), P("col"))
    return jax.shard_map(
        on_device, mesh=mesh, in_specs=in_specs, out_specs=out_specs, check_vma=False
    )
```

profile of v0, /device:TPU:0, one launch (start us, length us, event | category | flops | bytes accessed | tf_op | source)
XLA Modules:
  0.0 484.3 jit_solution(17791880367086263619)
XLA Ops:
  8.0 0.0 all-gather.9.cloned.1.call-start
  8.0 1.4 fusion.28
  10.1 1.7 constant_dynamic-slice_fusion.3
  11.8 0.0 all-gather.9.cloned.1.call-update
  11.8 0.0 all-reduce.3.cloned.1.call-start
  14.5 1.3 fusion.27
  15.7 6.9 %convolution_select_fusion.1 = f32[3840,512]{1,0:T(8,128)} fusion(pred[]{:T(512)S(6)} %eq.59, f32[3840,1920]{1,0:T(8,128)} %param.4, s32[]{:T(128)S(6)} %select_n.140, bf16[1,512,512]{2,1,0:T(8,128)(2,1)S(1)} %get-tuple-element.4, s32[]{:T(128)S(6)} %select_n.142), kind=kOutput, calls=%fused_computation.6 | convolution fusion | flops 3021864960 | bytes 9961481 | tf_op jit(solution)/shard_map/dot_general | solution.py:11
  22.6 0.0 all-reduce.3.cloned.1.call-update
  22.7 0.0 all-gather.5.cloned.1.call-start
  22.7 2.3 constant_dynamic-slice_fusion.2
  25.0 0.0 all-gather.5.cloned.1.call-update
  25.0 0.0 all-gather.11.cloned.1.call-start
  28.5 0.7 broadcast_compare_fusion
  29.2 0.7 fusion.15
  29.9 12.8 %all-gather.9.cloned.1.call-done = f32[512,512]{1,0:T(8,128)} async-done(((f32[128,512]{1,0:T(8,128)}), f32[512,512]{1,0:T(8,128)}) %all-gather.9.cloned.1.call-update) | async-done | bytes 1048592 | tf_op jit(solution)/shard_map/all_gather | solution.py:65
  42.6 103.8 %all-reduce.3.cloned.1.call-done = f32[3840,512]{1,0:T(8,128)} async-done(((f32[3840,512]{1,0:T(8,128)}), f32[3840,512]{1,0:T(8,128)}) %all-reduce.3.cloned.1.call-update) | async-done | bytes 7864336 | tf_op jit(solution)/shard_map/psum | solution.py:70
  146.4 16.6 %multiply_subtract_fusion.1 = f32[3840,512]{1,0:T(8,128)S(1)} fusion(f32[3840,512]{1,0:T(8,128)} %param.5, f32[3840,512]{1,0:T(8,128)} %all-reduce.3.cloned.1.call-done, f32[512,512]{1,0:T(8,128)} %all-gather.9.cloned.1.call-done, f32[3840]{0:T(1024)S(1)} %fusion.15), kind=kOutput, calls=%fused_computation.4 | convolution fusion | flops 12083527680 | bytes 24656896 | tf_op jit(solution)/shard_map/dot_general | solution.py:11
  163.0 0.0 copy-start
  163.0 3.2 copy-done
  166.2 0.7 constant_dynamic-slice_fusion
  167.0 0.0 all-gather.11.cloned.1.call-update
  167.0 0.2 all-reduce.5.cloned.1.call-start
  167.2 11.9 %broadcast.286.clone = f32[3840,1920]{1,0:T(8,128)} broadcast(f32[]{:T(128)} %constant.140.clone.1), dimensions={} | broadcast | bytes 29491204 | tf_op jit(solution)/shard_map/broadcast.6
  179.1 3.1 dynamic-slice_dynamic-update-slice_fusion.1
  182.2 0.0 all-gather.5.cloned.1.call-done
  182.2 61.2 %subtract_select_fusion = f32[3840,1920]{1,0:T(8,128)} fusion(f32[3840,1920]{1,0:T(8,128)} %dynamic-slice_dynamic-update-slice_fusion.1, f32[3840,1920]{1,0:T(8,128)} %param.4, f32[3840,512]{1,0:T(8,128)} %all-reduce.3.cloned.1.call-done, f32[3840]{0:T(1024)S(1)} %fusion.15, pred[1920]{0:T(1024)(128)(4,1)S(1)} %convert_compare_fusion, ...), kind=kOutput, calls=%fused_computation.1 | convolution fusion | flops 45328957440 | bytes 100298880 | tf_op jit(solution)/shard_map/dot_general | solution.py:11
  243.4 6.9 %convolution_select_fusion = f32[3840,512]{1,0:T(8,128)} fusion(pred[]{:T(512)S(6)} %eq.56, f32[3840,1920]{1,0:T(8,128)} %subtract_select_fusion, s32[]{:T(128)S(6)} %select_n.146, bf16[1,512,512]{2,1,0:T(8,128)(2,1)S(1)} %get-tuple-element.3, s32[]{:T(128)S(6)} %select_n.142), kind=kOutput, calls=%fused_computation.5 | convolution fusion | flops 3021864960 | bytes 9961481 | tf_op jit(solution)/shard_map/dot_general | solution.py:11
  250.3 0.0 all-reduce.5.cloned.1.call-update
  250.3 0.3 all-gather.7.cloned.1.call-start
  250.6 2.2 constant_dynamic-slice_fusion.1
  252.8 0.0 all-gather.7.cloned.1.call-update
  252.9 1.3 broadcast_compare_fusion.1
  254.2 1.3 fusion.14
  255.6 0.0 all-gather.11.cloned.1.call-done
  255.6 115.9 %all-reduce.5.cloned.1.call-done = f32[3840,512]{1,0:T(8,128)} async-done(((f32[3840,512]{1,0:T(8,128)}), f32[3840,512]{1,0:T(8,128)}) %all-reduce.5.cloned.1.call-update) | async-done | bytes 7864336 | tf_op jit(solution)/shard_map/psum | solution.py:70
  371.5 17.8 %multiply_reduce_fusion = (f32[512]{0:T(512)S(1)}, f32[3840,512]{1,0:T(8,128)}) fusion(f32[3840,512]{1,0:T(8,128)} %copy-done, f32[3840,512]{1,0:T(8,128)} %all-reduce.5.cloned.1.call-done, f32[512,512]{1,0:T(8,128)} %all-gather.11.cloned.1.call-done, f32[3840]{0:T(1024)S(1)} %fusion.14), kind=kOutput, calls=%fused_computation.2 | convolution fusion | flops 12087459840 | bytes 24658944 | tf_op jit(solution)/shard_map/dot_general | solution.py:11
  389.2 11.7 %psum.23 = f32[512]{0:T(512)S(1)} all-reduce(f32[512]{0:T(512)S(1)} %get-tuple-element.7), channel_id=1, replica_groups=mesh['row'=4,'col'=8] {'row'}, use_global_device_ids=true, to_apply=%region_3.4 | all-reduce | flops 512 | bytes 4096 | tf_op jit(solution)/shard_map/psum | solution.py:79
  400.9 0.6 add_sqrt_fusion
  401.5 11.6 %broadcast.286 = f32[3840,1920]{1,0:T(8,128)} broadcast(f32[]{:T(128)} %constant.140.clone.1), dimensions={} | broadcast | bytes 29491204 | tf_op jit(solution)/shard_map/broadcast.6
  413.1 3.1 dynamic-slice_dynamic-update-slice_fusion
  416.2 0.0 all-gather.7.cloned.1.call-done
  416.2 60.9 %select_convert_fusion = bf16[3840,1920]{1,0:T(8,128)(2,1)} fusion(f32[3840,1920]{1,0:T(8,128)} %dynamic-slice_dynamic-update-slice_fusion, f32[3840,1920]{1,0:T(8,128)} %subtract_select_fusion, f32[3840,512]{1,0:T(8,128)} %all-reduce.5.cloned.1.call-done, f32[3840]{0:T(1024)S(1)} %fusion.14, pred[1920]{0:T(1024)(128)(4,1)S(1)} %convert_compare_fusion.1, ...), kind=kOutput, calls=%fused_computation | convolution fusion | flops 45328957440 | bytes 85553280 | tf_op jit(solution)/shard_map/dot_general | solution.py:11
  (4 shorter events, 0.0 us)
Async XLA Ops:
  8.0 34.6 %all-gather.9.cloned.1.call-start = ((), (), s32[]{:S(2)}) async-start(), calls=%async_computation.4 | async-start | bytes 1310720 | tf_op jit(solution)/shard_map/all_gather | solution.py:65
  11.8 134.6 %all-reduce.3.cloned.1.call-start = ((), (), s32[]{:S(2)}) async-start(), calls=%async_computation | async-start | bytes 15728640 | tf_op jit(solution)/shard_map/psum | solution.py:70
  22.7 159.5 %all-gather.5.cloned.1.call-start = ((), (), s32[]{:S(2)}) async-start(), calls=%async_computation.1 | async-start | bytes 4915200 | tf_op jit(solution)/shard_map/all_gather | solution.py:64
  25.0 230.5 %all-gather.11.cloned.1.call-start = ((), (), s32[]{:S(2)}) async-start(), calls=%async_computation.5 | async-start | bytes 1310720 | tf_op jit(solution)/shard_map/all_gather | solution.py:65
  163.0 3.2 copy-start
  167.0 204.5 %all-reduce.5.cloned.1.call-start = ((), (), s32[]{:S(2)}) async-start(), calls=%async_computation.2 | async-start | bytes 15728640 | tf_op jit(solution)/shard_map/psum | solution.py:70
  250.3 165.9 %all-gather.7.cloned.1.call-start = ((), (), s32[]{:S(2)}) async-start(), calls=%async_computation.3 | async-start | bytes 4915200 | tf_op jit(solution)/shard_map/all_gather | solution.py:64
Sparse Core Ops, SparseCore 0:
  11.9 30.6 all-gather.8
  44.2 75.7 all-gather.4
  167.1 28.0 all-gather.10
  253.0 76.5 all-gather.6
Sparse Core Ops, SparseCore 1:
  22.7 123.6 all-reduce.2
  250.4 121.0 all-reduce.4
where the time goes:
time: 485 us; the launch traced here: 484 us
  waiting for transfers between devices  233 us (48%)
  matrix products  170 us (35%)
  local copies, waits for them, and re-layouts  42.5 us (9%)
  between operations  22 us (5%)
  blocking collectives  11.7 us (2%)
    psum x2, waiting for transfers between devices, on_device(): multipliers = lax.psum(partial_value, 'col')  220 us
    dot_general x6, matrix products, product(): jnp.dot(first, second, precision=lax.Precision.HIGHEST, preferred_element...  170 us
    another operation x2, local copies, waits for them, and re-layouts  23.5 us
    all_gather x2, waiting for transfers between devices, on_device(): lax.all_gather(rhs_piece, 'row', axis=0, tiled=True)  12.8 us
    psum x1, blocking collectives, on_device(): totals = lax.psum(jnp.sum(right_sides * right_sides, axis=0), 'row')  11.7 us
  transfers between devices with their start and end apart: 6, of which 3 were waited for; matrix products, arithmetic and copies ran while one was open for 31% of the time, Pallas kernels for 0%

commit v1 on v0

--- a/solution.py
+++ b/solution.py
@@ -67,7 +67,17 @@
         inverse = pivot_inverses[section].astype(jnp.float32)
         own_rows = cut_along(inverse, col_index % row_count * block_size, block_size, 0)
         partial_value = jnp.where(is_owner, product(column_slab, own_rows), 0.0)
-        multipliers = lax.psum(partial_value, "col")
+        slots = lax.axis_size("col")
+        multipliers, long_array = (partial_value, 0)
+        while 1 << long_array < slots:
+            history = []
+            tick = 0
+            while tick < slots:
+                history.append((tick, tick ^ 1 << long_array))
+                tick += 1
+            low = lax.ppermute(multipliers, "col", history)
+            multipliers = multipliers + low
+            long_array = long_array + 1
         own_mult = cut_along(multipliers, col_index % row_count * block_size, block_size, 1)
         placed = lax.dynamic_update_slice_in_dim(
             jnp.zeros_like(current), own_mult, panel_id // group_count * block_size, 1

time: 485 us -> 986 us (2.03)
  waiting for transfers between devices: 233 us -> 667 us
  other arithmetic: 4.61 us -> 61.6 us
    ppermute x0 -> x6, waiting for transfers between devices: none -> 667 us  [on_device(): low = lax.ppermute(multipliers, 'col', history)]
    psum x2 -> x0, waiting for transfers between devices: 220 us -> none  [on_device(): multipliers = lax.psum(partial_value, 'col')]
    add x0 -> x6, other arithmetic: none -> 57 us  [on_device(): multipliers = multipliers + low]
    all_gather x2, waiting for transfers between devices: 12.8 us -> 0.02 us  [on_device(): lax.all_gather(rhs_piece, 'row', axis=0, tiled=True)]
  transfers between devices with their start and end apart: 6 -> 10, of which waited for: 3 -> 6; matrix products, arithmetic and copies ran while one was open for 31% -> 11% of each run, Pallas kernels for 0% -> 0%
where the time goes in v1:
time: 986 us; the launch traced here: 979 us
  waiting for transfers between devices  667 us (68%)
  matrix products  166 us (17%)
  other arithmetic  61.6 us (6%)
  local copies, waits for them, and re-layouts  42.2 us (4%)
  between operations  20.9 us (2%)
  blocking collectives  12.1 us (1%)
    ppermute x6, waiting for transfers between devices, on_device(): low = lax.ppermute(multipliers, 'col', history)  667 us
    dot_general x6, matrix products, product(): jnp.dot(first, second, precision=lax.Precision.HIGHEST, preferred_element...  166 us
    add x6, other arithmetic, on_device(): multipliers = multipliers + low  57 us
    another operation x2, local copies, waits for them, and re-layouts  23.2 us
  transfers between devices with their start and end apart: 10, of which 6 were waited for; matrix products, arithmetic and copies ran while one was open for 11% of the time, Pallas kernels for 0%

profile of v1, /device:TPU:0, one launch (start us, length us, event | category | flops | bytes accessed | tf_op | source)
XLA Modules:
  0.0 979.1 jit_solution(10929267179223101930)
XLA Ops:
  7.2 0.0 all-gather.5.cloned.1.call-start
  7.2 1.4 fusion.28
  11.2 1.3 fusion.27
  12.6 4.8 convolution_select_fusion.1
  17.4 0.6 collective-permute-start
  17.9 12.2 %collective-permute-done = f32[3840,512]{1,0:T(8,128)} collective-permute-done((f32[3840,512]{1,0:T(8,128)S(1)}, f32[3840,512]{1,0:T(8,128)}, u32[]{:S(2)}, u32[]{:S(2)}) %collective-permute-start) | collective-permute-done | bytes 7864352 | tf_op jit(solution)/shard_map/ppermute | solution.py:78
  30.1 8.4 add.100
  38.5 2.8 collective-permute-start.1
  41.3 169.7 %collective-permute-done.1 = f32[3840,512]{1,0:T(8,128)S(1)} collective-permute-done((f32[3840,512]{1,0:T(8,128)}, f32[3840,512]{1,0:T(8,128)S(1)}, u32[]{:S(2)}, u32[]{:S(2)}) %collective-permute-start.1) | collective-permute-done | bytes 7864352 | tf_op jit(solution)/shard_map/ppermute | solution.py:78
  211.1 8.4 add.101
  219.5 1.8 collective-permute-start.2
  221.9 2.2 constant_dynamic-slice_fusion.2
  224.1 0.0 all-gather.5.cloned.1.call-update
  224.2 0.2 all-gather.9.cloned.1.call-start
  227.2 0.7 broadcast_compare_fusion
  227.9 0.7 fusion.15
  228.5 162.0 %collective-permute-done.2 = f32[3840,512]{1,0:T(8,128)} collective-permute-done((f32[3840,512]{1,0:T(8,128)}, f32[3840,512]{1,0:T(8,128)}, u32[]{:S(2)}, u32[]{:S(2)}) %collective-permute-start.2) | collective-permute-done | bytes 7864352 | tf_op jit(solution)/shard_map/ppermute | solution.py:78
  390.5 10.6 %add.102 = f32[3840,512]{1,0:T(8,128)} add(f32[3840,512]{1,0:T(8,128)} %add.101, f32[3840,512]{1,0:T(8,128)} %collective-permute-done.2) | non-fusion elementwise | flops 1966080 | bytes 23592960 | tf_op jit(solution)/shard_map/add | solution.py:79
  401.1 11.6 %broadcast.286.clone = f32[3840,1920]{1,0:T(8,128)} broadcast(f32[]{:T(128)} %constant.140.clone.1), dimensions={} | broadcast | bytes 29491204 | tf_op jit(solution)/shard_map/broadcast.6
  412.8 3.1 dynamic-slice_dynamic-update-slice_fusion.1
  415.9 0.0 all-gather.5.cloned.1.call-done
  415.9 61.1 %subtract_select_fusion = f32[3840,1920]{1,0:T(8,128)} fusion(f32[3840,1920]{1,0:T(8,128)} %dynamic-slice_dynamic-update-slice_fusion.1, f32[3840,1920]{1,0:T(8,128)} %param.4, f32[3840,512]{1,0:T(8,128)} %add.102, f32[3840]{0:T(1024)S(1)} %fusion.15, pred[1920]{0:T(1024)(128)(4,1)S(1)} %convert_compare_fusion, ...), kind=kOutput, calls=%fused_computation.1 | convolution fusion | flops 45328957440 | bytes 100298880 | tf_op jit(solution)/shard_map/dot_general | solution.py:11
  477.0 4.8 convolution_select_fusion
  481.8 0.1 collective-permute-start.3
  481.9 12.5 %collective-permute-done.3 = f32[3840,512]{1,0:T(8,128)} collective-permute-done((f32[3840,512]{1,0:T(8,128)S(1)}, f32[3840,512]{1,0:T(8,128)}, u32[]{:S(2)}, u32[]{:S(2)}) %collective-permute-start.3) | collective-permute-done | bytes 7864352 | tf_op jit(solution)/shard_map/ppermute | solution.py:78
  494.4 8.4 add.105
  502.8 1.5 collective-permute-start.4
  504.3 1.7 constant_dynamic-slice_fusion.3
  506.0 0.0 all-gather.9.cloned.1.call-update
  506.0 0.4 all-gather.11.cloned.1.call-start
  506.4 168.0 %collective-permute-done.4 = f32[3840,512]{1,0:T(8,128)} collective-permute-done((f32[3840,512]{1,0:T(8,128)}, f32[3840,512]{1,0:T(8,128)}, u32[]{:S(2)}, u32[]{:S(2)}) %collective-permute-start.4) | collective-permute-done | bytes 7864352 | tf_op jit(solution)/shard_map/ppermute | solution.py:78
  674.4 10.6 %add.106 = f32[3840,512]{1,0:T(8,128)} add(f32[3840,512]{1,0:T(8,128)} %add.105, f32[3840,512]{1,0:T(8,128)} %collective-permute-done.4) | non-fusion elementwise | flops 1966080 | bytes 23592960 | tf_op jit(solution)/shard_map/add | solution.py:79
  685.1 1.5 collective-permute-start.5
  687.2 0.0 all-gather.9.cloned.1.call-done
  687.3 16.6 %multiply_subtract_fusion.1 = f32[3840,512]{1,0:T(8,128)S(1)} fusion(f32[3840,512]{1,0:T(8,128)} %param.5, f32[3840,512]{1,0:T(8,128)} %add.102, f32[512,512]{1,0:T(8,128)} %all-gather.9.cloned.1.call-done, f32[3840]{0:T(1024)S(1)} %fusion.15), kind=kOutput, calls=%fused_computation.4 | convolution fusion | flops 12083527680 | bytes 24656896 | tf_op jit(solution)/shard_map/dot_general | solution.py:11
  703.9 0.0 copy-start
  703.9 3.2 copy-done
  707.1 0.7 constant_dynamic-slice_fusion
  707.8 0.0 all-gather.11.cloned.1.call-update
  707.9 0.0 all-gather.7.cloned.1.call-start
  707.9 2.2 constant_dynamic-slice_fusion.1
  710.1 0.0 all-gather.7.cloned.1.call-update
  710.2 1.3 broadcast_compare_fusion.1
  711.6 1.3 fusion.14
  712.9 142.9 %collective-permute-done.5 = f32[3840,512]{1,0:T(8,128)} collective-permute-done((f32[3840,512]{1,0:T(8,128)}, f32[3840,512]{1,0:T(8,128)}, u32[]{:S(2)}, u32[]{:S(2)}) %collective-permute-start.5) | collective-permute-done | bytes 7864352 | tf_op jit(solution)/shard_map/ppermute | solution.py:78
  855.8 10.5 %add.107 = f32[3840,512]{1,0:T(8,128)} add(f32[3840,512]{1,0:T(8,128)} %add.106, f32[3840,512]{1,0:T(8,128)} %collective-permute-done.5) | non-fusion elementwise | flops 1966080 | bytes 23592960 | tf_op jit(solution)/shard_map/add | solution.py:79
  866.3 0.0 all-gather.11.cloned.1.call-done
  866.3 17.8 %multiply_reduce_fusion = (f32[512]{0:T(512)S(1)}, f32[3840,512]{1,0:T(8,128)}) fusion(f32[3840,512]{1,0:T(8,128)} %copy-done, f32[3840,512]{1,0:T(8,128)} %add.107, f32[512,512]{1,0:T(8,128)} %all-gather.11.cloned.1.call-done, f32[3840]{0:T(1024)S(1)} %fusion.14), kind=kOutput, calls=%fused_computation.2 | convolution fusion | flops 12087459840 | bytes 24658944 | tf_op jit(solution)/shard_map/dot_general | solution.py:11
  884.0 12.1 %psum.7 = f32[512]{0:T(512)S(1)} all-reduce(f32[512]{0:T(512)S(1)} %get-tuple-element.7), channel_id=1, replica_groups=mesh['row'=4,'col'=8] {'row'}, use_global_device_ids=true, to_apply=%region_1.2 | all-reduce | flops 512 | bytes 4096 | tf_op jit(solution)/shard_map/psum | solution.py:89
  896.1 0.6 add_sqrt_fusion
  896.7 11.6 %broadcast.286 = f32[3840,1920]{1,0:T(8,128)} broadcast(f32[]{:T(128)} %constant.140.clone.1), dimensions={} | broadcast | bytes 29491204 | tf_op jit(solution)/shard_map/broadcast.6
  908.3 3.1 dynamic-slice_dynamic-update-slice_fusion
  911.4 0.0 all-gather.7.cloned.1.call-done
  911.4 60.9 %select_convert_fusion = bf16[3840,1920]{1,0:T(8,128)(2,1)} fusion(f32[3840,1920]{1,0:T(8,128)} %dynamic-slice_dynamic-update-slice_fusion, f32[3840,1920]{1,0:T(8,128)} %subtract_select_fusion, f32[3840,512]{1,0:T(8,128)} %add.107, f32[3840]{0:T(1024)S(1)} %fusion.14, pred[1920]{0:T(1024)(128)(4,1)S(1)} %convert_compare_fusion.1, ...), kind=kOutput, calls=%fused_computation | convolution fusion | flops 45328957440 | bytes 85553280 | tf_op jit(solution)/shard_map/dot_general | solution.py:11
  (4 shorter events, 0.0 us)
Async XLA Ops:
  7.2 408.7 %all-gather.5.cloned.1.call-start = ((), (), s32[]{:S(2)}) async-start(), calls=%async_computation | async-start | bytes 4915200 | tf_op jit(solution)/shard_map/all_gather | solution.py:64
  17.4 12.7 %collective-permute-start = (f32[3840,512]{1,0:T(8,128)S(1)}, f32[3840,512]{1,0:T(8,128)}, u32[]{:S(2)}, u32[]{:S(2)}) collective-permute-start(f32[3840,512]{1,0:T(8,128)S(1)} %convolution_select_fusion.1), channel_id=1, source_target_pairs={{0,1},{1,0},{2,3},{3,2},{4,5},{5,4},{6,7},{7,6},{8,9},{9,8},{10,11... | collective-permute-start | bytes 23592968 | tf_op jit(solution)/shard_map/ppermute | solution.py:78
  38.5 172.6 %collective-permute-start.1 = (f32[3840,512]{1,0:T(8,128)}, f32[3840,512]{1,0:T(8,128)S(1)}, u32[]{:S(2)}, u32[]{:S(2)}) collective-permute-start(f32[3840,512]{1,0:T(8,128)} %add.100), channel_id=1, source_target_pairs={{0,2},{1,3},{2,0},{3,1},{4,6},{5,7},{6,4},{7,5},{8,10},{9,11},{10,... | collective-permute-start | bytes 23592968 | tf_op jit(solution)/shard_map/ppermute | solution.py:78
  219.5 171.0 %collective-permute-start.2 = (f32[3840,512]{1,0:T(8,128)}, f32[3840,512]{1,0:T(8,128)}, u32[]{:S(2)}, u32[]{:S(2)}) collective-permute-start(f32[3840,512]{1,0:T(8,128)} %add.101), channel_id=1, source_target_pairs={{0,4},{1,5},{2,6},{3,7},{4,0},{5,1},{6,2},{7,3},{8,12},{9,13},{10,... | collective-permute-start | bytes 23592968 | tf_op jit(solution)/shard_map/ppermute | solution.py:78
  224.2 463.1 %all-gather.9.cloned.1.call-start = ((), (), s32[]{:S(2)}) async-start(), calls=%async_computation.2 | async-start | bytes 1310720 | tf_op jit(solution)/shard_map/all_gather | solution.py:65
  481.8 12.6 %collective-permute-start.3 = (f32[3840,512]{1,0:T(8,128)S(1)}, f32[3840,512]{1,0:T(8,128)}, u32[]{:S(2)}, u32[]{:S(2)}) collective-permute-start(f32[3840,512]{1,0:T(8,128)S(1)} %convolution_select_fusion), channel_id=1, source_target_pairs={{0,1},{1,0},{2,3},{3,2},{4,5},{5,4},{6,7},{7,6},{8,9},{9,8},{10,11... | collective-permute-start | bytes 23592968 | tf_op jit(solution)/shard_map/ppermute | solution.py:78
  502.8 171.6 %collective-permute-start.4 = (f32[3840,512]{1,0:T(8,128)}, f32[3840,512]{1,0:T(8,128)}, u32[]{:S(2)}, u32[]{:S(2)}) collective-permute-start(f32[3840,512]{1,0:T(8,128)} %add.105), channel_id=1, source_target_pairs={{0,2},{1,3},{2,0},{3,1},{4,6},{5,7},{6,4},{7,5},{8,10},{9,11},{10,... | collective-permute-start | bytes 23592968 | tf_op jit(solution)/shard_map/ppermute | solution.py:78
  506.0 360.3 %all-gather.11.cloned.1.call-start = ((), (), s32[]{:S(2)}) async-start(), calls=%async_computation.3 | async-start | bytes 1310720 | tf_op jit(solution)/shard_map/all_gather | solution.py:65
  685.1 170.7 %collective-permute-start.5 = (f32[3840,512]{1,0:T(8,128)}, f32[3840,512]{1,0:T(8,128)}, u32[]{:S(2)}, u32[]{:S(2)}) collective-permute-start(f32[3840,512]{1,0:T(8,128)} %add.106), channel_id=1, source_target_pairs={{0,4},{1,5},{2,6},{3,7},{4,0},{5,1},{6,2},{7,3},{8,12},{9,13},{10,... | collective-permute-start | bytes 23592968 | tf_op jit(solution)/shard_map/ppermute | solution.py:78
  703.9 3.2 copy-start
  707.9 203.6 %all-gather.7.cloned.1.call-start = ((), (), s32[]{:S(2)}) async-start(), calls=%async_computation.1 | async-start | bytes 4915200 | tf_op jit(solution)/shard_map/all_gather | solution.py:64
Sparse Core Ops, SparseCore 0:
  224.3 76.6 all-gather.4
  506.1 28.2 all-gather.8
  708.0 28.2 all-gather.10
  737.7 75.7 all-gather.6
